TPU v7x, 256 devices: a whole 4x4x8 slice. The times are simulated.
256 devices in a mesh: grp: 16 (over z_lo, y, core), seq: 16 (over z_hi, x).
Axes of the slice: x: 4, y: 4, z: 8 (z_hi: 4, z_lo: 2; z = z_hi * 2 + z_lo), core: 2. Of those that a mesh axis runs over, the one named last changes fastest.
Arguments:
- query: bfloat16 [16, 4096, 640], P('grp', 'seq'), may hold values from -64 to 64
- resp_kv: bfloat16 [16, 4096, 256], P('grp', 'seq'), may hold values from -6 to 6
- prompt_kv: bfloat16 [16, 4096, 256], P('grp', 'seq'), may hold values from -64 to 64
- grad_out: bfloat16 [16, 4096, 640], P('grp', 'seq'), may hold values from -6 to 6
- rewards: float32 [16, 16], P('grp'), may hold values from -4 to 4
- lengths: int32 [16, 16], P('grp'), may hold values from 1 to 256, as said below
- block_order: int32 [16, 32], P('grp'), may hold values from 0 to 31, each once within a row
Outputs:
- grad_query: bfloat16 [16, 4096, 640], P('grp', 'seq')
- grad_stream: bfloat16 [16, 4096, 256], P('grp', 'seq')
- grad_prompt: bfloat16 [16, 4096, 256], P('grp', 'seq')
Inputs may be any that keep to these rules, and one draw needn't show every extreme that they name: `lengths`: each response has 1 to 256 tokens; some response has exactly 256. Each row of block_order names every response block of its group once.
All inputs are finite; a program needn't handle non-finite values.
Results may differ from a plain program's by a relative error of at most 0.015.
Values may be sent and summed in bfloat16 or wider, within the bound.
A program may use at most 128 MiB of HBM per device.

v0:
```python
from functools import partial
import jax
import jax.numpy as jnp
from jax import lax
from jax.sharding import Mesh
from jax.sharding import PartitionSpec as P

RESP = 16
BLK = 128
NB = 2
SEQ = ("seq_0", "seq_1")
LOSS_SCALE = 32.0
BIG_NEGATIVE = -1e30


def in_one_piece(arrays, axis, dim, along):
    widths = [a.shape[along] for a in arrays]
    both = jnp.concatenate(arrays, axis=along)
    filled = lax.all_gather(both, axis, axis=dim, tiled=True)
    return tuple(jnp.split(filled, [sum(widths[:k]) for k in range(1, len(widths))], axis=along))


def reduced_to_own(blocks, axes, sequence):
    inside = blocks.shape[1:]
    blocks = blocks.reshape(*(lax.axis_size(a) for a in axes), *inside)
    blocks = jnp.moveaxis(blocks, sequence, range(len(axes))).reshape(-1, *inside)
    for k in sequence:
        blocks = lax.psum_scatter(blocks, axes[k], scatter_dimension=0, tiled=True)
    return blocks[0]


def split_up(value, dim, size):
    dims = value.shape
    blocks = value.reshape(*dims[:dim], size, dims[dim] // size, *dims[dim + 1 :])
    return jnp.moveaxis(blocks, dim, 0)


def sum_by_axis(value, axes, sequence, dim):
    size = lax.axis_size(axes)
    return reduced_to_own(split_up(value, dim, size), axes, sequence)


def product(pattern, first_operand, second_operand):
    return jnp.einsum(pattern, first_operand, second_operand, preferred_element_type=jnp.float32)


def block_terms(query_block, weighted, prompt_pairs, own_pairs, positions):
    half_width = prompt_pairs.shape[1] // 2
    score_scale = half_width ** (-0.5)
    prompt_keys = prompt_pairs[:, :half_width]
    prompt_values = prompt_pairs[:, half_width:]
    own_keys = own_pairs[:, :half_width]
    own_values = own_pairs[:, half_width:]
    visible = (jnp.arange(own_pairs.shape[0], dtype=jnp.int32)[None, :] <= positions[:, None])[None]
    scores_prompt = product("thd,kd->htk", query_block, prompt_keys) * score_scale
    scores_own = jnp.where(
        visible, product("thd,kd->htk", query_block, own_keys) * score_scale, BIG_NEGATIVE
    )
    peak_score = jnp.maximum(jnp.max(scores_prompt, axis=2), jnp.max(scores_own, axis=2))
    expo_prompt = jnp.exp(scores_prompt - peak_score[..., None])
    expo_own = jnp.where(visible, jnp.exp(scores_own - peak_score[..., None]), 0.0)
    prob_total = jnp.sum(expo_prompt, axis=2) + jnp.sum(expo_own, axis=2)
    probs_prompt = expo_prompt / prob_total[..., None]
    probs_own = expo_own / prob_total[..., None]
    low_prompt = probs_prompt.astype(jnp.bfloat16)
    low_own = probs_own.astype(jnp.bfloat16)
    attended = product("htk,kd->thd", low_prompt, prompt_values) + product(
        "htk,kd->thd", low_own, own_values
    )
    row_delta = jnp.einsum("thd,thd->ht", weighted.astype(jnp.float32), attended)
    grad_prompt_scores = (
        probs_prompt * (product("thd,kd->htk", weighted, prompt_values) - row_delta[..., None])
    ).astype(jnp.bfloat16)
    grad_own_scores = (
        probs_own * (product("thd,kd->htk", weighted, own_values) - row_delta[..., None])
    ).astype(jnp.bfloat16)
    grad_query = (
        product("htk,kd->thd", grad_prompt_scores, prompt_keys)
        + product("htk,kd->thd", grad_own_scores, own_keys)
    ) * score_scale
    prompt_term = jnp.concatenate(
        [
            product("htk,thd->kd", grad_prompt_scores, query_block) * score_scale,
            product("htk,thd->kd", low_prompt, weighted),
        ],
        axis=1,
    )
    own_term = jnp.concatenate(
        [
            product("htk,thd->kd", grad_own_scores, query_block) * score_scale,
            product("htk,thd->kd", low_own, weighted),
        ],
        axis=1,
    )
    return (grad_query, prompt_term, own_term, peak_score, prob_total, row_delta)


def local(query, resp_kv, prompt_kv, grad_out, rewards, lengths, block_order):
    head_width = resp_kv.shape[2] // 2
    head_count = query.shape[2] // head_width
    row_count = query.shape[1]
    local_blocks = row_count // BLK
    capacity = NB * BLK
    group_count = lax.axis_size("grp")
    seq_count = lax.axis_size(SEQ)
    count = lax.psum(jnp.sum(lengths[0]).astype(jnp.float32), "grp")
    advantage = rewards[0] - jnp.mean(rewards[0])
    factor = advantage * (LOSS_SCALE * group_count * RESP * capacity) / count
    block_plan = block_order[0]
    inverse = jnp.argsort(block_plan)
    prompt_all, stream_all = in_one_piece((prompt_kv[0], resp_kv[0]), SEQ, 0, 1)
    blocks = stream_all.reshape(block_plan.shape[0], BLK, 2 * head_width)
    stored = lax.axis_index(SEQ) * local_blocks + jnp.arange(local_blocks, dtype=jnp.int32)
    stream_block = block_plan[stored]
    response = stream_block // NB
    positions = (stream_block % NB)[:, None] * BLK + jnp.arange(BLK, dtype=jnp.int32)[None, :]
    token_weight = jnp.where(
        positions < lengths[0][response][:, None], factor[response][:, None], 0.0
    )
    weighted = (
        grad_out[0].reshape(local_blocks, BLK, head_count * head_width).astype(jnp.float32)
        * token_weight[..., None]
    ).astype(jnp.bfloat16)
    weighted = weighted.reshape(local_blocks, BLK, head_count, head_width)
    queries = query[0].reshape(local_blocks, BLK, head_count, head_width)
    slot_table = inverse.reshape(RESP, NB)[response]
    block_items = (queries, weighted, slot_table, positions)

    def block_step(with_prompt, carried, block_item):
        prompt_sum, stream_sum = carried
        query_block, weight_block, slot_index, block_positions = block_item
        own_pairs = jnp.take(blocks, slot_index, axis=0).reshape(capacity, 2 * head_width)
        grad_query, prompt_term, own_term, peak_score, prob_total, row_delta = block_terms(
            query_block, weight_block, prompt_all, own_pairs, block_positions
        )
        stream_sum = stream_sum.at[slot_index].add(own_term.reshape(NB, BLK, 2 * head_width))
        prompt_sum = prompt_sum + prompt_term
        return (
            (prompt_sum, stream_sum),
            (grad_query.astype(jnp.bfloat16), peak_score, prob_total, row_delta),
        )

    stream_zero = jnp.zeros((block_plan.shape[0], BLK, 2 * head_width), jnp.float32)
    initial = (jnp.zeros((prompt_all.shape[0], 2 * head_width), jnp.float32), stream_zero)
    (prompt_sum, stream_sum), block_outputs = lax.scan(
        partial(block_step, True), initial, block_items
    )
    prompt_grad = sum_by_axis(prompt_sum.astype(jnp.bfloat16), SEQ, (1, 0), 0).astype(jnp.float32)
    grad_rows = block_outputs[0]
    outgoing = stream_sum.reshape(seq_count, local_blocks * BLK, 2 * head_width)
    incoming = lax.all_to_all(
        outgoing.astype(jnp.bfloat16), SEQ, split_axis=0, concat_axis=0, tiled=True
    ).astype(outgoing.dtype)
    stream_grad = jnp.sum(incoming, axis=0)
    grad_query = grad_rows.reshape(row_count, head_count * head_width)
    return (
        grad_query[None],
        stream_grad.astype(jnp.bfloat16)[None],
        prompt_grad.astype(jnp.bfloat16)[None],
    )


def solution(mesh):
    split = Mesh(mesh.devices.reshape(mesh.shape["grp"], 4, 4), ("grp", "seq_0", "seq_1"))
    placed = (
        P("grp", SEQ, None),
        P("grp", SEQ, None),
        P("grp", SEQ, None),
        P("grp", SEQ, None),
        P("grp", None),
        P("grp", None),
        P("grp", None),
    )
    return jax.shard_map(
        local,
        mesh=split,
        in_specs=placed,
        out_specs=(P("grp", SEQ, None), P("grp", SEQ, None), P("grp", SEQ, None)),
        check_vma=False,
    )
```

profile of v0, /device:TPU:2, one launch (start us, length us, event | category | flops | bytes accessed | tf_op | source)
XLA Modules:
  0.0 268.5 jit_solution(16111596052325326619)
XLA Ops:
  7.2 1.7 pad_maximum_fusion.1
  9.0 1.3 reduce_sum.49
  10.9 32.3 %psum.7 = f32[]{:T(128)} all-reduce(f32[]{:T(128)S(6)} %convert_element_type.45), channel_id=1, replica_groups=mesh['grp'=16,'seq_0'=4,'seq_1'=4] {'grp'}, use_global_device_ids=true, to_apply=%region_2.0 | all-reduce | flops 1 | bytes 8 | tf_op jit(solution)/shard_map/psum | solution.py:106
  43.2 2.3 sort.17
  45.5 1.3 gather_fusion.1
  46.8 1.3 reduce_sum.48
  48.7 1.2 divide_bitcast_fusion
  50.6 1.3 gather_fusion.3
  52.5 1.3 reshape.311
  55.7 1.5 copy.35
  57.3 31.1 %all-gather.2.cloned.1.call-done = bf16[4096,512]{1,0:T(8,128)(2,1)} async-done(((bf16[256,512]{1,0:T(8,128)(2,1)}), bf16[4096,512]{1,0:T(8,128)(2,1)}) %all-gather.2.cloned.1.call-update) | async-done | bytes 4194320 | tf_op jit(solution)/shard_map/all_gather | solution.py:19
  88.4 3.8 %fusion.75 = (bf16[4096,256]{1,0:T(8,128)(2,1)}, bf16[4096,256]{1,0:T(8,128)(2,1)S(1)}) fusion(bf16[4096,512]{1,0:T(8,128)(2,1)} %all-gather.2.cloned.1.call-done), kind=kLoop, calls=%fused_computation.118 | loop fusion | bytes 8388608 | tf_op jit(solution)/shard_map/split | solution.py:20
  92.1 2.5 broadcast_in_dim.81
  94.6 73.7 %while.15 = (s32[]{:T(128)}, f32[4096,256]{0,1:T(8,128)}, f32[32,128,256]{2,1,0:T(8,128)}, bf16[2,128,5,128]{3,1,2,0:T(8,128)(2,1)}, bf16[2,128,5,128]{3,1,2,0:T...) while((s32[]{:T(128)}, f32[4096,256]{0,1:T(8,128)}, ...), condition=%wide.region_10.11_spmd.clone, body=%wide.region_4.10_spmd.clone.sunk | while | flops 4335778816 | bytes 192303536 | solution.py:145
  94.8 2.8 %gather_fusion = bf16[2,128,256]{2,1,0:T(8,128)(2,1)S(1)} fusion(bf16[32,128,256]{2,1,0:T(8,128)(2,1)} %get-tuple-element.235, s32[1024]{0:T(1024)S(1)} %pad_clamp_fusion.4), kind=kCustom, calls=%fused_computation.clone.clone.1 | custom fusion | bytes 262152 | tf_op jit(solution)/shard_map/while/body/eval_jaxpr/jit(_take)/gather | solution.py:132
  97.9 1.6 bitcast_reduce_fusion.2
  99.7 1.8 fusion.129
  101.5 1.4 convolution_bitcast_fusion.12
  103.5 2.2 fusion.131
  105.8 1.4 fusion.132
  107.1 1.2 fusion.135
  108.8 5.6 %convolution_bitcast_fusion.11 = f32[4096,128]{0,1:T(8,128)S(1)} fusion(bf16[2,128,5,128]{3,1,2,0:T(8,128)(2,1)} %get-tuple-element.236, s32[]{:T(128)S(6)} %copy.69, f32[128,5,4096]{2,0,1:T(8,128)} %copy-done, f32[5,128]{1,0:T(8,128)S(1)} %add.189, f32[5,128]{1,0:T(8,128)S(1)} %max.9), kind=kOutput, calls=%fused_computation.14.clone.1 | convolution fusion | flops 681574400 | bytes 12751876 | tf_op jit(solution)/shard_map/while/body/eval_jaxpr/htk,thd->kd/dot_general | solution.py:44
  114.6 1.2 slice-done.2
  115.8 4.4 %fusion.133 = bf16[5,128,4096]{2,1,0:T(8,128)(2,1)S(1)} fusion(f32[5,128]{1,0:T(8,128)S(1)} %fusion.132, bf16[4096,256]{1,0:T(8,128)(2,1)} %copy-done.1, bf16[2,128,5,128]{3,1,2,0:T(8,128)(2,1)} %get-tuple-element.236, s32[]{:T(128)S(6)} %copy.69, f32[5,128]{1,0:T(8,128)S(1)} %add.189, f32[5,128]{1,0:T(8,128)S(1)} %max.9, ...), kind=kOutput, calls=%fused_computation.8.clone.1 | convolution fusion | flops 686817280 | bytes 16948740 | tf_op jit(solution)/shard_map/while/body/eval_jaxpr/thd,kd->htk/dot_general | solution.py:44
  120.2 2.7 %convolution_bitcast_fusion.13 = f32[128,5,128]{2,0,1:T(8,128)S(1)} fusion(bf16[5,128,4096]{2,1,0:T(8,128)(2,1)S(1)} %fusion.133, bf16[4096,256]{1,0:T(8,128)(2,1)} %copy-done.1), kind=kOutput, calls=%fused_computation.36.clone.1 | convolution fusion | flops 671088640 | bytes 6619136 | tf_op jit(solution)/shard_map/while/body/eval_jaxpr/htk,kd->thd/dot_general | solution.py:44
  125.1 2.9 %maximum_add_fusion.2 = f32[4096,256]{0,1:T(8,128)} fusion(f32[4096,128]{0,1:T(8,128)S(1)} %convolution_bitcast_fusion.11, f32[4096,128]{0,1:T(8,128)S(1)} %fusion.134, f32[4096,256]{0,1:T(8,128)} %get-tuple-element.216, pred[]{:T(512)S(6)} %compare.21), kind=kLoop, calls=%fused_computation.17.clone.1 | loop fusion | flops 3145728 | bytes 12582913 | tf_op jit(solution)/shard_map/while/body/eval_jaxpr/add | solution.py:137
  128.0 2.3 scatter_fusion
  130.4 2.8 %gather_fusion = bf16[2,128,256]{2,1,0:T(8,128)(2,1)S(1)} fusion(bf16[32,128,256]{2,1,0:T(8,128)(2,1)} %get-tuple-element.235, s32[1024]{0:T(1024)S(1)} %pad_clamp_fusion.4), kind=kCustom, calls=%fused_computation.clone.clone.1 | custom fusion | bytes 262152 | tf_op jit(solution)/shard_map/while/body/eval_jaxpr/jit(_take)/gather | solution.py:132
  133.6 1.6 bitcast_reduce_fusion.2
  135.3 1.8 fusion.129
  137.2 1.4 convolution_bitcast_fusion.12
  139.2 2.2 fusion.131
  141.4 1.4 fusion.132
  142.8 1.2 fusion.135
  144.5 5.6 %convolution_bitcast_fusion.11 = f32[4096,128]{0,1:T(8,128)S(1)} fusion(bf16[2,128,5,128]{3,1,2,0:T(8,128)(2,1)} %get-tuple-element.236, s32[]{:T(128)S(6)} %copy.69, f32[128,5,4096]{2,0,1:T(8,128)} %copy-done, f32[5,128]{1,0:T(8,128)S(1)} %add.189, f32[5,128]{1,0:T(8,128)S(1)} %max.9), kind=kOutput, calls=%fused_computation.14.clone.1 | convolution fusion | flops 681574400 | bytes 12751876 | tf_op jit(solution)/shard_map/while/body/eval_jaxpr/htk,thd->kd/dot_general | solution.py:44
  150.3 1.2 slice-done.2
  151.5 4.4 %fusion.133 = bf16[5,128,4096]{2,1,0:T(8,128)(2,1)S(1)} fusion(f32[5,128]{1,0:T(8,128)S(1)} %fusion.132, bf16[4096,256]{1,0:T(8,128)(2,1)} %copy-done.1, bf16[2,128,5,128]{3,1,2,0:T(8,128)(2,1)} %get-tuple-element.236, s32[]{:T(128)S(6)} %copy.69, f32[5,128]{1,0:T(8,128)S(1)} %add.189, f32[5,128]{1,0:T(8,128)S(1)} %max.9, ...), kind=kOutput, calls=%fused_computation.8.clone.1 | convolution fusion | flops 686817280 | bytes 16948740 | tf_op jit(solution)/shard_map/while/body/eval_jaxpr/thd,kd->htk/dot_general | solution.py:44
  155.9 2.7 %convolution_bitcast_fusion.13 = f32[128,5,128]{2,0,1:T(8,128)S(1)} fusion(bf16[5,128,4096]{2,1,0:T(8,128)(2,1)S(1)} %fusion.133, bf16[4096,256]{1,0:T(8,128)(2,1)} %copy-done.1), kind=kOutput, calls=%fused_computation.36.clone.1 | convolution fusion | flops 671088640 | bytes 6619136 | tf_op jit(solution)/shard_map/while/body/eval_jaxpr/htk,kd->thd/dot_general | solution.py:44
  160.8 5.2 %maximum_add_fusion.2 = f32[4096,256]{0,1:T(8,128)} fusion(f32[4096,128]{0,1:T(8,128)S(1)} %convolution_bitcast_fusion.11, f32[4096,128]{0,1:T(8,128)S(1)} %fusion.134, f32[4096,256]{0,1:T(8,128)} %get-tuple-element.216, pred[]{:T(512)S(6)} %compare.21), kind=kLoop, calls=%fused_computation.17.clone.1 | loop fusion | flops 3145728 | bytes 12582913 | tf_op jit(solution)/shard_map/while/body/eval_jaxpr/add | solution.py:137
  166.0 2.3 scatter_fusion
  168.3 2.5 convert_element_type.49
  170.7 2.8 %reshape_reshape.3 = bf16[4,4,256,256]{2,1,0,3:T(4,128)(2,1)} reshape(bf16[4096,256]{0,1:T(8,128)(2,1)S(1)} %convert_element_type.49) | data formatting | bytes 4194304 | tf_op jit(solution)/shard_map/reshape;reshape | solution.py:25
  173.5 4.3 %copy.37 = bf16[4,4,256,256]{3,2,0,1:T(8,128)(2,1)} copy(bf16[4,4,256,256]{2,1,0,3:T(4,128)(2,1)} %reshape_reshape.3) | data formatting | bytes 4194304 | tf_op jit(solution)/shard_map/reshape;reshape | solution.py:25
  177.9 3.8 %convert_element_type.47 = bf16[32,128,256]{2,1,0:T(8,128)(2,1)} convert(f32[32,128,256]{2,1,0:T(8,128)} %get-tuple-element.60) | non-fusion elementwise | flops 1048576 | bytes 6291456 | tf_op jit(solution)/shard_map/convert_element_type | solution.py:152
  181.7 9.1 %all-to-all-start = ((bf16[16,256,256]{2,1,0:T(8,128)(2,1)}), bf16[16,256,256]{2,1,0:T(8,128)(2,1)S(1)}, u32[]{:S(2)}, u32[]{:S(2)}) async-start(bf16[16,256,256]{2,1,0:T(8,128)(2,1)} %bitcast.11), calls=%async_computation | async-start | bytes 4194304 | tf_op jit(solution)/shard_map/all_to_all | solution.py:151
  190.9 37.1 %reduce-scatter.3.cloned.1.call-done = bf16[4,256,256]{2,1,0:T(8,128)(2,1)} async-done(((bf16[16,256,256]{2,1,0:T(8,128)(2,1)}), bf16[4,256,256]{2,1,0:T(8,128)(2,1)}) %reduce-scatter.3.cloned.1.call-update) | async-done | bytes 524304 | tf_op jit(solution)/shard_map/reduce_scatter | solution.py:28
  229.4 10.1 %all-to-all-done = bf16[16,256,256]{2,1,0:T(8,128)(2,1)S(1)} async-done(((bf16[16,256,256]{2,1,0:T(8,128)(2,1)}), bf16[16,256,256]{2,1,0:T(8,128)(2,1)S(1)}, u32[]{:S(2)}, u32[]{:S(2)}) %all-to-all-start) | async-done | bytes 2097184 | tf_op jit(solution)/shard_map/all_to_all | solution.py:151
  240.4 21.5 %reduce-scatter.5.cloned.1.call-done = bf16[1,256,256]{2,1,0:T(8,128)(2,1)} async-done(((bf16[4,256,256]{2,1,0:T(8,128)(2,1)}), bf16[1,256,256]{2,1,0:T(8,128)(2,1)}) %reduce-scatter.5.cloned.1.call-update) | async-done | bytes 131088 | tf_op jit(solution)/shard_map/reduce_scatter | solution.py:28
  (92 shorter events, 13.5 us)
Async XLA Ops:
  7.2 81.2 %all-gather.2.cloned.1.call-start = ((), (), s32[]{:S(2)}) async-start(), calls=%async_computation.3 | async-start | bytes 4456448 | tf_op jit(solution)/shard_map/all_gather | solution.py:19
  8.9 219.1 %reduce-scatter.3.cloned.1.call-start = ((), (), s32[]{:S(2)}) async-start(), calls=%async_computation.4 | async-start | bytes 2621440 | tf_op jit(solution)/shard_map/reduce_scatter | solution.py:28
  94.6 11.1 %copy-start.1 = (bf16[4096,256]{1,0:T(8,128)(2,1)}, bf16[4096,256]{1,0:T(8,128)(2,1)S(1)}, u32[]{:S(2)}) copy-start(bf16[4096,256]{1,0:T(8,128)(2,1)S(1)} %get-tuple-element.232) | copy-start | bytes 6291460 | tf_op jit(solution)/shard_map/while
  99.5 4.0 %copy-start = (f32[128,5,4096]{2,0,1:T(8,128)}, f32[128,5,4096]{2,0,1:T(8,128)S(1)}, u32[]{:S(2)}) copy-start(f32[128,5,4096]{2,0,1:T(8,128)S(1)} %get-tuple-element.199) | copy-start | bytes 31457284 | tf_op jit(solution)/shard_map/while
  108.6 5.8 %slice-start = ((s8[10485760]{0:T(1024)(128)(4,1)}), s8[2097152]{0:T(1024)(128)(4,1)S(1)}, s32[]{:S(2)}) async-start(s8[10485760]{0:T(1024)(128)(4,1)} %bitcast.268), calls=%async_computation.6 | async-start | bytes 4194304 | tf_op jit(solution)/shard_map/while
  108.8 5.8 %slice-start.1 = ((s8[10485760]{0:T(1024)(128)(4,1)}), s8[4194304]{0:T(1024)(128)(4,1)S(1)}, s32[]{:S(2)}) async-start(s8[10485760]{0:T(1024)(128)(4,1)} %bitcast.268), calls=%async_computation.7 | async-start | bytes 8388608 | tf_op jit(solution)/shard_map/while
  108.8 7.0 %slice-start.2 = ((s8[10485760]{0:T(1024)(128)(4,1)}), s8[4194304]{0:T(1024)(128)(4,1)S(1)}, s32[]{:S(2)}) async-start(s8[10485760]{0:T(1024)(128)(4,1)} %bitcast.268), calls=%async_computation.8 | async-start | bytes 8388608 | tf_op jit(solution)/shard_map/while
  122.9 1.1 copy-start.3
  124.4 0.7 copy-start.4
  125.1 5.2 %copy-start.2 = (bf16[4096,256]{1,0:T(8,128)(2,1)S(1)}, bf16[4096,256]{1,0:T(8,128)(2,1)}, u32[]{:S(2)}) copy-start(bf16[4096,256]{1,0:T(8,128)(2,1)} %copy-done.1) | copy-start | bytes 6291460 | tf_op jit(solution)/shard_map/while
  130.3 11.1 %copy-start.1 = (bf16[4096,256]{1,0:T(8,128)(2,1)}, bf16[4096,256]{1,0:T(8,128)(2,1)S(1)}, u32[]{:S(2)}) copy-start(bf16[4096,256]{1,0:T(8,128)(2,1)S(1)} %get-tuple-element.232) | copy-start | bytes 6291460 | tf_op jit(solution)/shard_map/while
  135.2 4.0 %copy-start = (f32[128,5,4096]{2,0,1:T(8,128)}, f32[128,5,4096]{2,0,1:T(8,128)S(1)}, u32[]{:S(2)}) copy-start(f32[128,5,4096]{2,0,1:T(8,128)S(1)} %get-tuple-element.199) | copy-start | bytes 31457284 | tf_op jit(solution)/shard_map/while
  144.3 5.8 %slice-start = ((s8[10485760]{0:T(1024)(128)(4,1)}), s8[2097152]{0:T(1024)(128)(4,1)S(1)}, s32[]{:S(2)}) async-start(s8[10485760]{0:T(1024)(128)(4,1)} %bitcast.268), calls=%async_computation.6 | async-start | bytes 4194304 | tf_op jit(solution)/shard_map/while
  144.5 5.8 %slice-start.1 = ((s8[10485760]{0:T(1024)(128)(4,1)}), s8[4194304]{0:T(1024)(128)(4,1)S(1)}, s32[]{:S(2)}) async-start(s8[10485760]{0:T(1024)(128)(4,1)} %bitcast.268), calls=%async_computation.7 | async-start | bytes 8388608 | tf_op jit(solution)/shard_map/while
  144.5 7.0 %slice-start.2 = ((s8[10485760]{0:T(1024)(128)(4,1)}), s8[4194304]{0:T(1024)(128)(4,1)S(1)}, s32[]{:S(2)}) async-start(s8[10485760]{0:T(1024)(128)(4,1)} %bitcast.268), calls=%async_computation.8 | async-start | bytes 8388608 | tf_op jit(solution)/shard_map/while
  158.6 1.1 copy-start.3
  160.0 0.7 copy-start.4
  160.8 7.5 %copy-start.2 = (bf16[4096,256]{1,0:T(8,128)(2,1)S(1)}, bf16[4096,256]{1,0:T(8,128)(2,1)}, u32[]{:S(2)}) copy-start(bf16[4096,256]{1,0:T(8,128)(2,1)} %copy-done.1) | copy-start | bytes 6291460 | tf_op jit(solution)/shard_map/while
  177.9 50.2 %copy-start.5 = (bf16[2,128,5,128]{3,1,2,0:T(8,128)(2,1)S(1)}, bf16[2,128,5,128]{3,1,2,0:T(8,128)(2,1)}, u32[]{:S(2)}) copy-start(bf16[2,128,5,128]{3,1,2,0:T(8,128)(2,1)} %get-tuple-element.59) | copy-start | bytes 983044
  181.7 57.8 %all-to-all-start = ((bf16[16,256,256]{2,1,0:T(8,128)(2,1)}), bf16[16,256,256]{2,1,0:T(8,128)(2,1)S(1)}, u32[]{:S(2)}, u32[]{:S(2)}) async-start(bf16[16,256,256]{2,1,0:T(8,128)(2,1)} %bitcast.11), calls=%async_computation | async-start | bytes 4194304 | tf_op jit(solution)/shard_map/all_to_all | solution.py:151
  190.8 71.1 %reduce-scatter.5.cloned.1.call-start = ((), (), s32[]{:S(2)}) async-start(), calls=%async_computation.5 | async-start | bytes 655360 | tf_op jit(solution)/shard_map/reduce_scatter | solution.py:28
Sparse Core Ops, SparseCore 0:
  10.4 77.9 all-gather.1
  178.0 49.9 reduce-scatter.2
  231.1 30.7 reduce-scatter.4
where the time goes:
time: 269 us; the launch traced here: 268 us
  waiting for transfers between devices  99.8 us (37%)
  matrix products  45 us (17%)
  local copies, waits for them, and re-layouts  34.1 us (13%)
  other arithmetic  32.4 us (12%)
  blocking collectives  32.3 us (12%)
  between operations  15.1 us (6%)
  starting transfers between devices  9.26 us (3%)
    reduce_scatter x2, waiting for transfers between devices, reduced_to_own(): blocks = lax.psum_scatter(blocks, axes[k], scatter_dimension=0, tiled=True)  58.6 us
    dot_general x24, matrix products, product(): jnp.einsum(pattern, first_operand, second_operand, preferred_element_type...  45 us
    psum x1, blocking collectives, local(): count = lax.psum(jnp.sum(lengths[0]).astype(jnp.float32), 'grp')  32.3 us
    all_gather x1, waiting for transfers between devices, in_one_piece(): filled = lax.all_gather(both, axis, axis=dim, tiled=True)  31.1 us
    all_to_all x1, waiting for transfers between devices, local(): lax.all_to_all(outgoing.astype(jnp.bfloat16), SEQ, split_axis=0, concat_a...  10.1 us
    all_to_all x1, starting transfers between devices, local(): lax.all_to_all(outgoing.astype(jnp.bfloat16), SEQ, split_axis=0, concat_a...  9.15 us
    add x2, other arithmetic, block_step(): prompt_sum = prompt_sum + prompt_term  8.07 us
    another operation x2, local copies, waits for them, and re-layouts, reduced_to_own(): blocks = blocks.reshape(*(lax.axis_size(a) for a in axes), *inside)  7.1 us
  transfers between devices with their start and end apart: 4, of which 4 were waited for; matrix products, arithmetic and copies ran while one was open for 8% of the time, Pallas kernels for 0%

commit v1 on v0

--- a/solution.py
+++ b/solution.py
@@ -11,6 +11,11 @@
 SEQ = ("seq_0", "seq_1")
 LOSS_SCALE = 32.0
 BIG_NEGATIVE = -1e30
+
+
+def add_all(x, axis):
+    parts = lax.all_gather(x, axis)
+    return jnp.sum(parts, axis=0)
 
 
 def in_one_piece(arrays, axis, dim, along):
@@ -103,7 +108,7 @@
     capacity = NB * BLK
     group_count = lax.axis_size("grp")
     seq_count = lax.axis_size(SEQ)
-    count = lax.psum(jnp.sum(lengths[0]).astype(jnp.float32), "grp")
+    count = add_all(jnp.sum(lengths[0]).astype(jnp.float32), "grp")
     advantage = rewards[0] - jnp.mean(rewards[0])
     factor = advantage * (LOSS_SCALE * group_count * RESP * capacity) / count
     block_plan = block_order[0]

time: 269 us -> 270 us (level)
    unnamed x0 -> x1, blocking collectives: none -> 32.3 us
    psum x1 -> x0, blocking collectives: 32.3 us -> none  [local(): count = lax.psum(jnp.sum(lengths[0]).astype(jnp.float32), 'grp')]
  transfers between devices with their start and end apart: 4 -> 4, of which waited for: 4 -> 4; matrix products, arithmetic and copies ran while one was open for 8% -> 9% of each run, Pallas kernels for 0% -> 0%
where the time goes in v1:
time: 270 us; the launch traced here: 269 us
  waiting for transfers between devices  97.9 us (36%)
  matrix products  45.1 us (17%)
  local copies, waits for them, and re-layouts  36.1 us (13%)
  other arithmetic  33.2 us (12%)
  blocking collectives  32.3 us (12%)
  between operations  15.1 us (6%)
  starting transfers between devices  9.25 us (3%)
    reduce_scatter x2, waiting for transfers between devices, reduced_to_own(): blocks = lax.psum_scatter(blocks, axes[k], scatter_dimension=0, tiled=True)  60.2 us
    dot_general x24, matrix products, product(): jnp.einsum(pattern, first_operand, second_operand, preferred_element_type...  45.1 us
    unnamed x1, blocking collectives  32.3 us
    all_gather x1, waiting for transfers between devices, in_one_piece(): filled = lax.all_gather(both, axis, axis=dim, tiled=True)  29.2 us
    all_to_all x1, starting transfers between devices, local(): lax.all_to_all(outgoing.astype(jnp.bfloat16), SEQ, split_axis=0, concat_a...  9.13 us
    all_to_all x1, waiting for transfers between devices, local(): lax.all_to_all(outgoing.astype(jnp.bfloat16), SEQ, split_axis=0, concat_a...  8.42 us
    add x2, other arithmetic, block_step(): prompt_sum = prompt_sum + prompt_term  8.07 us
    another operation x2, local copies, waits for them, and re-layouts, reduced_to_own(): blocks = blocks.reshape(*(lax.axis_size(a) for a in axes), *inside)  7.1 us
  transfers between devices with their start and end apart: 4, of which 4 were waited for; matrix products, arithmetic and copies ran while one was open for 9% of the time, Pallas kernels for 0%

profile of v1, /device:TPU:2, one launch (start us, length us, event | category | flops | bytes accessed | tf_op | source)
XLA Modules:
  0.0 269.4 jit_solution(12663245096783217022)
XLA Ops:
  7.2 1.7 pad_maximum_fusion.1
  9.0 1.3 reduce_sum.58
  10.9 1.3 reduce_sum.57
  12.2 1.3 dynamic-slice
  14.2 32.3 %all-reduce = f32[16]{0:T(128)S(1)} all-reduce(f32[16]{0:T(128)S(1)} %dynamic-update-slice), channel_id=1, replica_groups=mesh['grp'=16,'seq_0'=4,'seq_1'=4] {'grp'}, use_global_device_ids=true, to_apply=%add | all-reduce | flops 16 | bytes 128
  47.3 2.3 sort.17
  49.5 1.3 gather_fusion.1
  51.4 1.3 divide_bitcast_fusion
  53.4 1.3 gather_fusion.3
  55.4 1.3 reshape.316
  58.6 1.5 copy.35
  60.1 29.2 %all-gather.2.cloned.1.call-done = bf16[4096,512]{1,0:T(8,128)(2,1)} async-done(((bf16[256,512]{1,0:T(8,128)(2,1)}), bf16[4096,512]{1,0:T(8,128)(2,1)}) %all-gather.2.cloned.1.call-update) | async-done | bytes 4194320 | tf_op jit(solution)/shard_map/all_gather | solution.py:24
  89.3 3.8 %fusion.75 = (bf16[4096,256]{1,0:T(8,128)(2,1)}, bf16[4096,256]{1,0:T(8,128)(2,1)S(1)}) fusion(bf16[4096,512]{1,0:T(8,128)(2,1)} %all-gather.2.cloned.1.call-done), kind=kLoop, calls=%fused_computation.118 | loop fusion | bytes 8388608 | tf_op jit(solution)/shard_map/split | solution.py:25
  93.1 2.5 broadcast_in_dim.81
  95.6 73.7 %while.15 = (s32[]{:T(128)}, f32[4096,256]{0,1:T(8,128)}, f32[32,128,256]{2,1,0:T(8,128)}, bf16[2,128,5,128]{3,1,2,0:T(8,128)(2,1)}, bf16[2,128,5,128]{3,1,2,0:T...) while((s32[]{:T(128)}, f32[4096,256]{0,1:T(8,128)}, ...), condition=%wide.region_10.11_spmd.clone, body=%wide.region_4.10_spmd.clone.sunk | while | flops 4335778816 | bytes 192303536 | solution.py:150
  95.7 2.8 %gather_fusion = bf16[2,128,256]{2,1,0:T(8,128)(2,1)S(1)} fusion(bf16[32,128,256]{2,1,0:T(8,128)(2,1)} %get-tuple-element.235, s32[1024]{0:T(1024)S(1)} %pad_clamp_fusion.4), kind=kCustom, calls=%fused_computation.clone.clone.1 | custom fusion | bytes 262152 | tf_op jit(solution)/shard_map/while/body/eval_jaxpr/jit(_take)/gather | solution.py:137
  98.9 1.6 bitcast_reduce_fusion.2
  100.7 1.8 fusion.129
  102.5 1.4 convolution_bitcast_fusion.12
  104.5 2.2 fusion.131
  106.7 1.4 fusion.132
  108.1 1.2 fusion.135
  109.8 5.6 %convolution_bitcast_fusion.11 = f32[4096,128]{0,1:T(8,128)S(1)} fusion(bf16[2,128,5,128]{3,1,2,0:T(8,128)(2,1)} %get-tuple-element.236, s32[]{:T(128)S(6)} %copy.70, f32[128,5,4096]{2,0,1:T(8,128)} %copy-done, f32[5,128]{1,0:T(8,128)S(1)} %add.189, f32[5,128]{1,0:T(8,128)S(1)} %max.9), kind=kOutput, calls=%fused_computation.14.clone.1 | convolution fusion | flops 681574400 | bytes 12751876 | tf_op jit(solution)/shard_map/while/body/eval_jaxpr/htk,thd->kd/dot_general | solution.py:49
  115.6 1.2 slice-done.2
  116.8 4.4 %fusion.133 = bf16[5,128,4096]{2,1,0:T(8,128)(2,1)S(1)} fusion(f32[5,128]{1,0:T(8,128)S(1)} %fusion.132, bf16[4096,256]{1,0:T(8,128)(2,1)} %copy-done.1, bf16[2,128,5,128]{3,1,2,0:T(8,128)(2,1)} %get-tuple-element.236, s32[]{:T(128)S(6)} %copy.70, f32[5,128]{1,0:T(8,128)S(1)} %add.189, f32[5,128]{1,0:T(8,128)S(1)} %max.9, ...), kind=kOutput, calls=%fused_computation.8.clone.1 | convolution fusion | flops 686817280 | bytes 16948740 | tf_op jit(solution)/shard_map/while/body/eval_jaxpr/thd,kd->htk/dot_general | solution.py:49
  121.2 2.7 %convolution_bitcast_fusion.13 = f32[128,5,128]{2,0,1:T(8,128)S(1)} fusion(bf16[5,128,4096]{2,1,0:T(8,128)(2,1)S(1)} %fusion.133, bf16[4096,256]{1,0:T(8,128)(2,1)} %copy-done.1), kind=kOutput, calls=%fused_computation.36.clone.1 | convolution fusion | flops 671088640 | bytes 6619136 | tf_op jit(solution)/shard_map/while/body/eval_jaxpr/htk,kd->thd/dot_general | solution.py:49
  126.1 2.9 %maximum_add_fusion.2 = f32[4096,256]{0,1:T(8,128)} fusion(f32[4096,128]{0,1:T(8,128)S(1)} %convolution_bitcast_fusion.11, f32[4096,128]{0,1:T(8,128)S(1)} %fusion.134, f32[4096,256]{0,1:T(8,128)} %get-tuple-element.216, pred[]{:T(512)S(6)} %compare.21), kind=kLoop, calls=%fused_computation.17.clone.1 | loop fusion | flops 3145728 | bytes 12582913 | tf_op jit(solution)/shard_map/while/body/eval_jaxpr/add | solution.py:142
  128.9 2.3 scatter_fusion
  131.4 2.8 %gather_fusion = bf16[2,128,256]{2,1,0:T(8,128)(2,1)S(1)} fusion(bf16[32,128,256]{2,1,0:T(8,128)(2,1)} %get-tuple-element.235, s32[1024]{0:T(1024)S(1)} %pad_clamp_fusion.4), kind=kCustom, calls=%fused_computation.clone.clone.1 | custom fusion | bytes 262152 | tf_op jit(solution)/shard_map/while/body/eval_jaxpr/jit(_take)/gather | solution.py:137
  134.6 1.6 bitcast_reduce_fusion.2
  136.3 1.8 fusion.129
  138.2 1.4 convolution_bitcast_fusion.12
  140.2 2.2 fusion.131
  142.4 1.4 fusion.132
  145.5 5.6 %convolution_bitcast_fusion.11 = f32[4096,128]{0,1:T(8,128)S(1)} fusion(bf16[2,128,5,128]{3,1,2,0:T(8,128)(2,1)} %get-tuple-element.236, s32[]{:T(128)S(6)} %copy.70, f32[128,5,4096]{2,0,1:T(8,128)} %copy-done, f32[5,128]{1,0:T(8,128)S(1)} %add.189, f32[5,128]{1,0:T(8,128)S(1)} %max.9), kind=kOutput, calls=%fused_computation.14.clone.1 | convolution fusion | flops 681574400 | bytes 12751876 | tf_op jit(solution)/shard_map/while/body/eval_jaxpr/htk,thd->kd/dot_general | solution.py:49
  151.2 1.2 slice-done.2
  152.4 4.4 %fusion.133 = bf16[5,128,4096]{2,1,0:T(8,128)(2,1)S(1)} fusion(f32[5,128]{1,0:T(8,128)S(1)} %fusion.132, bf16[4096,256]{1,0:T(8,128)(2,1)} %copy-done.1, bf16[2,128,5,128]{3,1,2,0:T(8,128)(2,1)} %get-tuple-element.236, s32[]{:T(128)S(6)} %copy.70, f32[5,128]{1,0:T(8,128)S(1)} %add.189, f32[5,128]{1,0:T(8,128)S(1)} %max.9, ...), kind=kOutput, calls=%fused_computation.8.clone.1 | convolution fusion | flops 686817280 | bytes 16948740 | tf_op jit(solution)/shard_map/while/body/eval_jaxpr/thd,kd->htk/dot_general | solution.py:49
  156.8 2.7 %convolution_bitcast_fusion.13 = f32[128,5,128]{2,0,1:T(8,128)S(1)} fusion(bf16[5,128,4096]{2,1,0:T(8,128)(2,1)S(1)} %fusion.133, bf16[4096,256]{1,0:T(8,128)(2,1)} %copy-done.1), kind=kOutput, calls=%fused_computation.36.clone.1 | convolution fusion | flops 671088640 | bytes 6619136 | tf_op jit(solution)/shard_map/while/body/eval_jaxpr/htk,kd->thd/dot_general | solution.py:49
  161.7 5.2 %maximum_add_fusion.2 = f32[4096,256]{0,1:T(8,128)} fusion(f32[4096,128]{0,1:T(8,128)S(1)} %convolution_bitcast_fusion.11, f32[4096,128]{0,1:T(8,128)S(1)} %fusion.134, f32[4096,256]{0,1:T(8,128)} %get-tuple-element.216, pred[]{:T(512)S(6)} %compare.21), kind=kLoop, calls=%fused_computation.17.clone.1 | loop fusion | flops 3145728 | bytes 12582913 | tf_op jit(solution)/shard_map/while/body/eval_jaxpr/add | solution.py:142
  166.9 2.3 scatter_fusion
  169.2 2.5 convert_element_type.49
  171.7 2.8 %reshape_reshape.3 = bf16[4,4,256,256]{2,1,0,3:T(4,128)(2,1)} reshape(bf16[4096,256]{0,1:T(8,128)(2,1)S(1)} %convert_element_type.49) | data formatting | bytes 4194304 | tf_op jit(solution)/shard_map/reshape;reshape | solution.py:30
  174.5 4.3 %copy.37 = bf16[4,4,256,256]{3,2,0,1:T(8,128)(2,1)} copy(bf16[4,4,256,256]{2,1,0,3:T(4,128)(2,1)} %reshape_reshape.3) | data formatting | bytes 4194304 | tf_op jit(solution)/shard_map/reshape;reshape | solution.py:30
  178.8 3.8 %convert_element_type.47 = bf16[32,128,256]{2,1,0:T(8,128)(2,1)} convert(f32[32,128,256]{2,1,0:T(8,128)} %get-tuple-element.60) | non-fusion elementwise | flops 1048576 | bytes 6291456 | tf_op jit(solution)/shard_map/convert_element_type | solution.py:157
  182.7 9.1 %all-to-all-start = ((bf16[16,256,256]{2,1,0:T(8,128)(2,1)}), bf16[16,256,256]{2,1,0:T(8,128)(2,1)S(1)}, u32[]{:S(2)}, u32[]{:S(2)}) async-start(bf16[16,256,256]{2,1,0:T(8,128)(2,1)} %bitcast.13), calls=%async_computation | async-start | bytes 4194304 | tf_op jit(solution)/shard_map/all_to_all | solution.py:156
  191.8 38.0 %reduce-scatter.3.cloned.1.call-done = bf16[4,256,256]{2,1,0:T(8,128)(2,1)} async-done(((bf16[16,256,256]{2,1,0:T(8,128)(2,1)}), bf16[4,256,256]{2,1,0:T(8,128)(2,1)}) %reduce-scatter.3.cloned.1.call-update) | async-done | bytes 524304 | tf_op jit(solution)/shard_map/reduce_scatter | solution.py:33
  231.2 8.4 %all-to-all-done = bf16[16,256,256]{2,1,0:T(8,128)(2,1)S(1)} async-done(((bf16[16,256,256]{2,1,0:T(8,128)(2,1)}), bf16[16,256,256]{2,1,0:T(8,128)(2,1)S(1)}, u32[]{:S(2)}, u32[]{:S(2)}) %all-to-all-start) | async-done | bytes 2097184 | tf_op jit(solution)/shard_map/all_to_all | solution.py:156
  240.6 22.3 %reduce-scatter.5.cloned.1.call-done = bf16[1,256,256]{2,1,0:T(8,128)(2,1)} async-done(((bf16[4,256,256]{2,1,0:T(8,128)(2,1)}), bf16[1,256,256]{2,1,0:T(8,128)(2,1)}) %reduce-scatter.5.cloned.1.call-update) | async-done | bytes 131088 | tf_op jit(solution)/shard_map/reduce_scatter | solution.py:33
  (96 shorter events, 16.2 us)
Async XLA Ops:
  7.2 82.2 %all-gather.2.cloned.1.call-start = ((), (), s32[]{:S(2)}) async-start(), calls=%async_computation.3 | async-start | bytes 4456448 | tf_op jit(solution)/shard_map/all_gather | solution.py:24
  8.9 220.9 %reduce-scatter.3.cloned.1.call-start = ((), (), s32[]{:S(2)}) async-start(), calls=%async_computation.4 | async-start | bytes 2621440 | tf_op jit(solution)/shard_map/reduce_scatter | solution.py:33
  95.6 11.1 %copy-start.1 = (bf16[4096,256]{1,0:T(8,128)(2,1)}, bf16[4096,256]{1,0:T(8,128)(2,1)S(1)}, u32[]{:S(2)}) copy-start(bf16[4096,256]{1,0:T(8,128)(2,1)S(1)} %get-tuple-element.232) | copy-start | bytes 6291460 | tf_op jit(solution)/shard_map/while
  100.5 4.0 %copy-start = (f32[128,5,4096]{2,0,1:T(8,128)}, f32[128,5,4096]{2,0,1:T(8,128)S(1)}, u32[]{:S(2)}) copy-start(f32[128,5,4096]{2,0,1:T(8,128)S(1)} %get-tuple-element.199) | copy-start | bytes 31457284 | tf_op jit(solution)/shard_map/while
  109.6 5.8 %slice-start = ((s8[10485760]{0:T(1024)(128)(4,1)}), s8[2097152]{0:T(1024)(128)(4,1)S(1)}, s32[]{:S(2)}) async-start(s8[10485760]{0:T(1024)(128)(4,1)} %bitcast.270), calls=%async_computation.6 | async-start | bytes 4194304 | tf_op jit(solution)/shard_map/while
  109.8 5.8 %slice-start.1 = ((s8[10485760]{0:T(1024)(128)(4,1)}), s8[4194304]{0:T(1024)(128)(4,1)S(1)}, s32[]{:S(2)}) async-start(s8[10485760]{0:T(1024)(128)(4,1)} %bitcast.270), calls=%async_computation.7 | async-start | bytes 8388608 | tf_op jit(solution)/shard_map/while
  109.8 7.0 %slice-start.2 = ((s8[10485760]{0:T(1024)(128)(4,1)}), s8[4194304]{0:T(1024)(128)(4,1)S(1)}, s32[]{:S(2)}) async-start(s8[10485760]{0:T(1024)(128)(4,1)} %bitcast.270), calls=%async_computation.8 | async-start | bytes 8388608 | tf_op jit(solution)/shard_map/while
  123.9 1.1 copy-start.3
  125.3 0.7 copy-start.4
  126.1 5.2 %copy-start.2 = (bf16[4096,256]{1,0:T(8,128)(2,1)S(1)}, bf16[4096,256]{1,0:T(8,128)(2,1)}, u32[]{:S(2)}) copy-start(bf16[4096,256]{1,0:T(8,128)(2,1)} %copy-done.1) | copy-start | bytes 6291460 | tf_op jit(solution)/shard_map/while
  131.3 11.1 %copy-start.1 = (bf16[4096,256]{1,0:T(8,128)(2,1)}, bf16[4096,256]{1,0:T(8,128)(2,1)S(1)}, u32[]{:S(2)}) copy-start(bf16[4096,256]{1,0:T(8,128)(2,1)S(1)} %get-tuple-element.232) | copy-start | bytes 6291460 | tf_op jit(solution)/shard_map/while
  136.2 4.0 %copy-start = (f32[128,5,4096]{2,0,1:T(8,128)}, f32[128,5,4096]{2,0,1:T(8,128)S(1)}, u32[]{:S(2)}) copy-start(f32[128,5,4096]{2,0,1:T(8,128)S(1)} %get-tuple-element.199) | copy-start | bytes 31457284 | tf_op jit(solution)/shard_map/while
  145.3 5.8 %slice-start = ((s8[10485760]{0:T(1024)(128)(4,1)}), s8[2097152]{0:T(1024)(128)(4,1)S(1)}, s32[]{:S(2)}) async-start(s8[10485760]{0:T(1024)(128)(4,1)} %bitcast.270), calls=%async_computation.6 | async-start | bytes 4194304 | tf_op jit(solution)/shard_map/while
  145.4 5.8 %slice-start.1 = ((s8[10485760]{0:T(1024)(128)(4,1)}), s8[4194304]{0:T(1024)(128)(4,1)S(1)}, s32[]{:S(2)}) async-start(s8[10485760]{0:T(1024)(128)(4,1)} %bitcast.270), calls=%async_computation.7 | async-start | bytes 8388608 | tf_op jit(solution)/shard_map/while
  145.5 7.0 %slice-start.2 = ((s8[10485760]{0:T(1024)(128)(4,1)}), s8[4194304]{0:T(1024)(128)(4,1)S(1)}, s32[]{:S(2)}) async-start(s8[10485760]{0:T(1024)(128)(4,1)} %bitcast.270), calls=%async_computation.8 | async-start | bytes 8388608 | tf_op jit(solution)/shard_map/while
  159.6 1.1 copy-start.3
  161.0 0.7 copy-start.4
  161.7 7.5 %copy-start.2 = (bf16[4096,256]{1,0:T(8,128)(2,1)S(1)}, bf16[4096,256]{1,0:T(8,128)(2,1)}, u32[]{:S(2)}) copy-start(bf16[4096,256]{1,0:T(8,128)(2,1)} %copy-done.1) | copy-start | bytes 6291460 | tf_op jit(solution)/shard_map/while
  178.8 51.0 %copy-start.5 = (bf16[2,128,5,128]{3,1,2,0:T(8,128)(2,1)S(1)}, bf16[2,128,5,128]{3,1,2,0:T(8,128)(2,1)}, u32[]{:S(2)}) copy-start(bf16[2,128,5,128]{3,1,2,0:T(8,128)(2,1)} %get-tuple-element.59) | copy-start | bytes 983044
  182.7 57.0 %all-to-all-start = ((bf16[16,256,256]{2,1,0:T(8,128)(2,1)}), bf16[16,256,256]{2,1,0:T(8,128)(2,1)S(1)}, u32[]{:S(2)}, u32[]{:S(2)}) async-start(bf16[16,256,256]{2,1,0:T(8,128)(2,1)} %bitcast.13), calls=%async_computation | async-start | bytes 4194304 | tf_op jit(solution)/shard_map/all_to_all | solution.py:156
  191.8 71.1 %reduce-scatter.5.cloned.1.call-start = ((), (), s32[]{:S(2)}) async-start(), calls=%async_computation.5 | async-start | bytes 655360 | tf_op jit(solution)/shard_map/reduce_scatter | solution.py:33
Sparse Core Ops, SparseCore 0:
  10.4 78.8 all-gather.1
  179.0 50.8 reduce-scatter.2
  232.9 29.9 reduce-scatter.4
